TPU v7x, 256 devices: a whole 4x4x8 slice. The times are simulated.
256 devices in a mesh: rep: 16 (over y_lo, x, core), blk: 16 (over z, y_hi).
Axes of the slice: x: 4, y: 4 (y_hi: 2, y_lo: 2; y = y_hi * 2 + y_lo), z: 8, core: 2. Of those that a mesh axis runs over, the one named last changes fastest.
Arguments:
- features: bfloat16 [2, 4096, 2048], P(None, 'rep'), may hold values from -0.125 to 0.125
- grad_act: bfloat16 [2, 4096, 24576], P(None, 'rep', 'blk'), may hold values from -2.5 to 2.5
- weights: bfloat16 [2048, 24576], P(None, 'blk'), may hold values from -6 to 6
- owner_slot: int32 [16, 48], P('blk'), may hold values from 0 to 47, each once within a row
- factors: float32 [16, 48, 2, 256, 256], P('blk', 'rep'), may hold values from -100 to 250, as said below
- roots: bfloat16 [16, 48, 2, 256, 256], P('blk', 'rep'), may hold values from -1 to 2, as said below
- helper_list: int32 [2, 16, 4], replicated, may hold values from 0 to 95, as said below
Outputs:
- weights_out: bfloat16 [16, 48, 256, 256], P('blk', 'rep')
- roots_out: bfloat16 [16, 48, 2, 256, 256], P('blk', 'rep')
Inputs may be any that keep to these rules, and one draw needn't show every extreme that they name: `owner_slot`: each row is a permutation of the slots of one group; slot s belongs to index s // 3 of rep. `factors`: symmetric positive definite. `roots`: Symmetric. `helper_list`: In a step every helper has exactly 4 ids, no id appears twice, and no helper has two ids of one group; a group has at most min(6, 16) of its ids in a step.
All inputs are finite; a program needn't handle non-finite values.
Results may differ from a plain program's by a relative error of at most 0.0085.
Values may be sent and summed in bfloat16 or wider, within the bound.
A program may use at most 128 MiB of HBM per device.

v0:
```python
import jax
import jax.numpy as jnp
from jax import lax
from jax.sharding import PartitionSpec as P

NEWTON = 3
RIDGE = 0.001
NORM_EPS = 1e-06
DECAY = 0.95
STEP_SIZE = 0.5


def exact_dot(first, second):
    return jnp.einsum("...ij,...jk->...ik", first, second)


def inverse_root(matrices):
    identity = jnp.eye(matrices.shape[-1], dtype=jnp.float32)
    ridged = matrices + RIDGE * identity
    norm_scale = jnp.sqrt(jnp.sum(ridged * ridged, axis=(-2, -1), keepdims=True) + NORM_EPS)
    current = ridged / norm_scale
    result = identity
    for newton_turn in range(NEWTON):
        factor = (5.0 * identity - current) / 4.0
        if newton_turn == 0:
            result = factor * norm_scale ** (-0.25)
        else:
            result = exact_dot(result, factor)
        if newton_turn + 1 < NEWTON:
            square = exact_dot(factor, factor)
            current = exact_dot(exact_dot(square, square), current)
    return result.astype(jnp.bfloat16)


def silu_slope(value):
    sigmoid = jax.nn.sigmoid(value)
    return sigmoid * (1.0 + value * (1.0 - sigmoid))


def body(features, grad_act, weights, owner_slot, factors, roots, helper_list):
    block_size = factors.shape[-1]
    owned = factors.shape[1]
    per_owner = 2 * owned
    slot_count = owner_slot.shape[1]
    token_count = features.shape[1]
    row_blocks = features.shape[2] // block_size
    col_blocks = grad_act.shape[2] // block_size
    rep_index = lax.axis_index("rep")
    blk_index = lax.axis_index("blk")
    slot_ids = jnp.arange(slot_count, dtype=jnp.int32)
    placing = owner_slot[0][None, :] == slot_ids[:, None]
    block_at = jnp.sum(jnp.where(placing, slot_ids[None, :], 0), axis=1)
    row_at = block_at // col_blocks
    column_pick = (
        (block_at % col_blocks)[:, None] == jnp.arange(col_blocks, dtype=jnp.int32)[None, :]
    ).astype(jnp.float32)
    mine = lax.dynamic_slice_in_dim(block_at, rep_index * owned, owned)
    grid = weights.reshape(row_blocks, block_size, col_blocks, block_size)
    own_weight = grid[mine // col_blocks, :, mine % col_blocks, :]
    current_factors = factors[0]
    current_roots = roots[0]
    owner_ids = blk_index * per_owner + jnp.arange(per_owner, dtype=jnp.int32)
    for step_index in range(features.shape[0]):
        features_now = features[step_index]
        feature_blocks = features_now.reshape(token_count, row_blocks, block_size)
        if step_index == 0:
            gate_value = jnp.dot(features_now, weights, preferred_element_type=jnp.float32)
        else:
            chosen = jnp.take(feature_blocks, row_at, axis=1)
            products = jnp.einsum(
                "tsa,sab->tsb",
                chosen,
                lax.all_gather(own_weight, "rep", axis=0, tiled=True),
                preferred_element_type=jnp.float32,
            )
            gate_value = jnp.einsum("tsb,sj->tjb", products, column_pick)
            gate_value = gate_value.reshape(token_count, col_blocks * block_size)
        dgate = (grad_act[step_index].astype(jnp.float32) * silu_slope(gate_value)).astype(
            jnp.bfloat16
        )
        dgate_blocks = dgate.reshape(token_count, col_blocks, block_size)
        left_rows = jnp.take(feature_blocks, block_at // col_blocks, axis=1)
        right_cols = jnp.take(dgate_blocks, block_at % col_blocks, axis=1)
        grads = lax.psum_scatter(
            jnp.einsum(
                "tsa,tsb->sab", left_rows, right_cols, preferred_element_type=jnp.float32
            ).astype(jnp.bfloat16),
            "rep",
            scatter_dimension=0,
            tiled=True,
        ).astype(jnp.float32)
        grads_low = grads.astype(jnp.bfloat16)
        left_side = jnp.einsum(
            "kij,kjl->kil", current_roots[:, 0], grads_low, preferred_element_type=jnp.float32
        ).astype(jnp.bfloat16)
        shaped = jnp.einsum(
            "kij,kjl->kil", left_side, current_roots[:, 1], preferred_element_type=jnp.float32
        )
        grad_norm = jnp.sqrt(jnp.sum(grads * grads, axis=(-2, -1), keepdims=True) + NORM_EPS)
        shaped_norm = jnp.sqrt(jnp.sum(shaped * shaped, axis=(-2, -1), keepdims=True) + NORM_EPS)
        stored_weight = lax.optimization_barrier(own_weight).astype(jnp.float32)
        own_weight = (stored_weight - STEP_SIZE * (grad_norm / shaped_norm) * shaped).astype(
            jnp.bfloat16
        )
        left_stat = exact_dot(grads, jnp.swapaxes(grads, -1, -2))
        right_stat = exact_dot(jnp.swapaxes(grads, -1, -2), grads)
        current_factors = DECAY * current_factors + (1.0 - DECAY) * jnp.stack(
            [left_stat, right_stat], axis=1
        )
        flat_factors = current_factors.reshape(per_owner, block_size, block_size)
        listing = helper_list[step_index]
        matches = listing[:, :, None] == owner_ids[None, None, :]
        sending = jnp.any(matches, axis=1).astype(jnp.float32)
        refreshed = jnp.sum(sending, axis=0)
        computed = inverse_root(flat_factors)
        previous = current_roots.reshape(per_owner, block_size, block_size)
        current_roots = jnp.where(refreshed[:, None, None] > 0.5, computed, previous).reshape(
            owned, 2, block_size, block_size
        )
    return (own_weight[None], current_roots[None])


def solution(mesh):
    return jax.shard_map(
        body,
        mesh=mesh,
        in_specs=(
            P(None, "rep", None),
            P(None, "rep", "blk"),
            P(None, "blk"),
            P("blk", None),
            P("blk", "rep", None, None, None),
            P("blk", "rep", None, None, None),
            P(),
        ),
        out_specs=(P("blk", "rep", None, None), P("blk", "rep", None, None, None)),
        check_vma=False,
    )
```

profile of v0, /device:TPU:32, one launch (start us, length us, event | category | flops | bytes accessed | tf_op | source)
XLA Modules:
  0.0 321.1 jit_solution(12098752500672347873)
XLA Ops:
  7.2 0.8 select_reduce_fusion
  8.0 1.7 fusion.168
  9.7 0.5 copy.159
  10.2 0.5 copy.125
  10.8 5.4 %fusion.46 = bf16[256,1536]{1,0:T(8,128)(2,1)S(1)} fusion(bf16[2048,1536]{1,0:T(8,128)(2,1)} %param.13, bf16[2,256,1536]{2,1,0:T(8,128)(2,1)} %param.12, bf16[2,256,2048]{2,1,0:T(8,128)(2,1)} %param.11), kind=kOutput, calls=%fused_computation.43 | convolution fusion | flops 1614544896 | bytes 8912896 | tf_op jit(solution)/shard_map/dot_general | solution.py:67
  16.2 1.2 copy.126
  17.3 1.4 copy.127
  18.7 4.8 %gather_fusion.1 = bf16[48,256,256]{2,1,0:T(8,128)(2,1)} fusion(bf16[256,8,256]{2,0,1:T(8,128)(2,1)S(1)} %copy.125, s32[1024]{0:T(1024)S(1)} %pad_clamp_fusion.1), kind=kCustom, calls=%fused_computation.clone | custom fusion | bytes 12583104 | tf_op jit(solution)/shard_map/jit(_take)/gather | solution.py:82
  23.5 4.9 %gather_fusion.2 = bf16[48,256,256]{2,1,0:T(8,128)(2,1)} fusion(bf16[256,6,256]{2,0,1:T(8,128)(2,1)S(1)} %copy.127, s32[1024]{0:T(1024)S(1)} %pad_clamp_fusion), kind=kCustom, calls=%fused_computation.1.clone | custom fusion | bytes 12583104 | tf_op jit(solution)/shard_map/jit(_take)/gather | solution.py:83
  28.5 9.8 %fusion.17 = bf16[48,256,256]{2,1,0:T(8,128)(2,1)} fusion(bf16[48,256,256]{2,1,0:T(8,128)(2,1)} %gather_fusion.2, pred[48]{0:T(512)(128)(4,1)S(1)} %get-tuple-element.19, bf16[48,256,256]{2,1,0:T(8,128)(2,1)} %gather_fusion.1, pred[48]{0:T(512)(128)(4,1)S(1)} %get-tuple-element.8), kind=kOutput, calls=%fused_computation.21 | convolution fusion | flops 1620049920 | bytes 18874464 | tf_op jit(solution)/shard_map/tsa,tsb->sab/dot_general | solution.py:85
  38.4 13.4 %reshape.265 = bf16[8,256,6,256]{3,2,1,0:T(8,128)(2,1)} reshape(bf16[2048,1536]{1,0:T(8,128)(2,1)} %param.13) | data formatting | bytes 12582912 | tf_op jit(solution)/shard_map/reshape | solution.py:58
  51.8 7.8 %copy.123 = bf16[8,256,6,256]{3,1,2,0:T(8,128)(2,1)} copy(bf16[8,256,6,256]{3,2,1,0:T(8,128)(2,1)} %reshape.265) | data formatting | bytes 12582912 | tf_op jit(solution)/shard_map/reshape | solution.py:58
  59.7 3.5 %gather_fusion = bf16[3,256,256]{2,1,0:T(8,128)(2,1)S(1)} fusion(bf16[8,256,6,256]{3,1,2,0:T(8,128)(2,1)} %copy.123, s32[3]{0:T(128)S(1)} %fusion.149), kind=kCustom, calls=%fused_computation.4 | custom fusion | bytes 786456 | tf_op jit(solution)/shard_map/gather | solution.py:59
  63.2 51.7 %reduce-scatter.3.cloned.1.call-done = bf16[3,256,256]{2,1,0:T(8,128)(2,1)} async-done(((bf16[48,256,256]{2,1,0:T(8,128)(2,1)}), bf16[3,256,256]{2,1,0:T(8,128)(2,1)}) %reduce-scatter.3.cloned.1.call-update) | async-done | bytes 393232 | tf_op jit(solution)/shard_map/reduce_scatter | solution.py:84
  114.9 1.2 multiply_reduce_fusion.4
  116.0 1.6 multiply_reduce_fusion.3
  117.7 0.9 subtract_convert_fusion.1
  118.9 0.5 copy.160
  119.4 0.5 copy.133
  119.9 4.9 %gather_fusion.3 = bf16[48,256,256]{2,1,0:T(8,128)(2,1)} fusion(bf16[256,8,256]{2,0,1:T(8,128)(2,1)S(1)} %copy.133, s32[1024]{0:T(1024)S(1)} %pad_clamp_fusion.1), kind=kCustom, calls=%fused_computation.2.clone | custom fusion | bytes 12583104 | tf_op jit(solution)/shard_map/jit(_take)/gather | solution.py:82
  125.4 36.9 %all-gather.2.cloned.1.call-done = bf16[48,256,256]{2,1,0:T(8,128)(2,1)} async-done(((bf16[3,256,256]{2,1,0:T(8,128)(2,1)}), bf16[48,256,256]{2,1,0:T(8,128)(2,1)}) %all-gather.2.cloned.1.call-update) | async-done | bytes 6291472 | tf_op jit(solution)/shard_map/all_gather | solution.py:73
  162.4 9.9 %fusion.14 = bf16[256,48,256]{0,2,1:T(8,128)(2,1)} fusion(bf16[48,256,256]{2,1,0:T(8,128)(2,1)} %all-gather.2.cloned.1.call-done, bf16[48,256,256]{2,1,0:T(8,128)(2,1)} %gather_fusion.3, pred[48]{0:T(512)(128)(4,1)S(1)} %get-tuple-element.8), kind=kOutput, calls=%fused_computation.20 | convolution fusion | flops 1613758464 | bytes 18874416 | tf_op jit(solution)/shard_map/tsa,sab->tsb/dot_general | solution.py:70
  172.3 8.9 %copy.136 = bf16[256,48,256]{2,1,0:T(8,128)(2,1)} copy(bf16[256,48,256]{0,2,1:T(8,128)(2,1)} %fusion.14) | data formatting | bytes 12582912 | tf_op jit(solution)/shard_map/tsa,sab->tsb/transpose | solution.py:70
  181.2 3.7 %fusion.144 = f32[6,256,256]{2,0,1:T(8,128)S(1)} fusion(bf16[256,48,256]{2,1,0:T(8,128)(2,1)} %copy.136, s32[48]{0:T(128)S(1)} %get-tuple-element.20), kind=kOutput, calls=%fused_computation.129 | convolution fusion | flops 37749024 | bytes 7864512 | tf_op jit(solution)/shard_map/tsb,sj->tjb/dot_general | solution.py:76
  184.9 0.8 fusion.55
  185.7 4.9 %gather_fusion.4 = bf16[48,256,256]{2,1,0:T(8,128)(2,1)} fusion(bf16[256,6,256]{2,0,1:T(8,128)(2,1)S(1)} %fusion.55, s32[1024]{0:T(1024)S(1)} %pad_clamp_fusion), kind=kCustom, calls=%fused_computation.3.clone | custom fusion | bytes 12583104 | tf_op jit(solution)/shard_map/jit(_take)/gather | solution.py:83
  190.6 9.7 %fusion.22 = bf16[48,256,256]{2,1,0:T(8,128)(2,1)} fusion(bf16[48,256,256]{2,1,0:T(8,128)(2,1)} %gather_fusion.4, pred[48]{0:T(512)(128)(4,1)S(1)} %get-tuple-element.19, bf16[48,256,256]{2,1,0:T(8,128)(2,1)} %gather_fusion.3, pred[48]{0:T(512)(128)(4,1)S(1)} %get-tuple-element.8), kind=kOutput, calls=%fused_computation.22 | convolution fusion | flops 1620049920 | bytes 18874464 | tf_op jit(solution)/shard_map/tsa,tsb->sab/dot_general | solution.py:85
  200.4 0.6 copy-done.9
  201.3 0.7 fusion.141
  202.9 1.3 copy.143
  204.1 70.8 %reduce-scatter.5.cloned.1.call-done = bf16[3,256,256]{2,1,0:T(8,128)(2,1)} async-done(((bf16[48,256,256]{2,1,0:T(8,128)(2,1)}), bf16[3,256,256]{2,1,0:T(8,128)(2,1)}) %reduce-scatter.5.cloned.1.call-update) | async-done | bytes 393232 | tf_op jit(solution)/shard_map/reduce_scatter | solution.py:84
  275.0 1.6 fusion.172
  276.9 0.9 fusion.45
  277.8 1.2 copy.141
  279.9 0.5 copy-done.7
  280.4 0.7 copy-done.3
  281.5 0.5 fusion.48
  282.0 1.8 fusion.32
  283.9 2.7 fusion.174
  286.5 5.1 %fusion.29 = bf16[6,256,256]{2,1,0:T(8,128)(2,1)} fusion(f32[6,256,256]{2,1,0:T(8,128)} %fusion.174, f32[256,256]{1,0:T(8,128)S(1)} %fusion.142), kind=kOutput, calls=%fused_computation.25 | convolution fusion | flops 403439616 | bytes 2621440 | tf_op jit(solution)/shard_map/...ij,...jk->...ik/dot_general | solution.py:14
  291.7 1.8 fusion.38
  293.5 2.7 fusion.171
  296.1 5.2 %fusion.35 = bf16[6,256,256]{2,1,0:T(8,128)(2,1)} fusion(f32[6,256,256]{2,1,0:T(8,128)} %fusion.171, f32[256,256]{1,0:T(8,128)S(1)} %fusion.142), kind=kOutput, calls=%fused_computation.29 | convolution fusion | flops 403439616 | bytes 2621440 | tf_op jit(solution)/shard_map/...ij,...jk->...ik/dot_general | solution.py:14
  301.3 4.1 %fusion.103 = bf16[6,256,256]{2,1,0:T(8,128)(2,1)} fusion(bf16[6,256,256]{2,1,0:T(8,128)(2,1)} %bitcast.159, bf16[6,256,256]{2,1,0:T(8,128)(2,1)} %fusion.35, f32[6,256,256]{2,1,0:T(8,128)} %fusion.171, f32[6,256,256]{2,1,0:T(8,128)S(1)} %get-tuple-element.13, f32[6]{0:T(128)S(1)} %power_multiply_fusion.1, f32[256,256]{1,0:T(8,128)S(1)} %fusion.142, ...), kind=kOutput, calls=%fused_computation.87 | convolution fusion | flops 607125504 | bytes 5767198 | tf_op jit(solution)/shard_map/...ij,...jk->...ik/dot_general | solution.py:14
  305.5 1.3 multiply_reduce_fusion.2
  306.8 2.5 multiply_reduce_fusion.1
  309.3 3.1 fusion.98
  312.5 2.1 fusion.140
  (55 shorter events, 3.7 us)
Async XLA Ops:
  7.2 107.7 %reduce-scatter.3.cloned.1.call-start = ((), (), s32[]{:S(2)}) async-start(), calls=%async_computation.2 | async-start | bytes 6684672 | tf_op jit(solution)/shard_map/reduce_scatter | solution.py:84
  38.3 124.0 %all-gather.2.cloned.1.call-start = ((), (), s32[]{:S(2)}) async-start(), calls=%async_computation.3 | async-start | bytes 6684672 | tf_op jit(solution)/shard_map/all_gather | solution.py:73
  38.4 13.4 %copy-start.5 = (bf16[1,3,2,256,256]{4,3,2,1,0:T(8,128)(2,1)S(1)}, bf16[1,3,2,256,256]{4,3,2,1,0:T(8,128)(2,1)}, u32[]{:S(2)}) copy-start(bf16[1,3,2,256,256]{4,3,2,1,0:T(8,128)(2,1)} %param.16) | copy-start | bytes 2359300
  118.6 156.3 %reduce-scatter.5.cloned.1.call-start = ((), (), s32[]{:S(2)}) async-start(), calls=%async_computation.4 | async-start | bytes 6684672 | tf_op jit(solution)/shard_map/reduce_scatter | solution.py:84
  119.9 4.9 %slice-start = ((bf16[2,256,1536]{2,1,0:T(8,128)(2,1)}), bf16[1,256,1536]{2,1,0:T(8,128)(2,1)S(1)}, s32[]{:S(2)}) async-start(bf16[2,256,1536]{2,1,0:T(8,128)(2,1)} %param.12), calls=%async_computation.5 | async-start | bytes 1572864 | tf_op jit(solution)/shard_map/slice | solution.py:78
  200.3 0.7 copy-start.9
  200.3 1.7 copy-start
  274.9 1.6 copy-start.2
  274.9 1.9 copy-start.6
  275.0 1.9 copy-start.8
  279.4 1.0 copy-start.7
  279.6 1.4 copy-start.3
  279.6 1.9 copy-start.4
  305.5 3.9 %copy-start.1 = (f32[6,256,256]{2,1,0:T(8,128)S(1)}, f32[6,256,256]{2,1,0:T(8,128)}, u32[]{:S(2)}) copy-start(f32[6,256,256]{2,1,0:T(8,128)} %fusion.174) | copy-start | bytes 4718596
Sparse Core Ops, SparseCore 0:
  38.4 76.3 reduce-scatter.2
  118.8 43.5 all-gather.1
  200.5 74.4 reduce-scatter.4
where the time goes:
time: 322 us; the launch traced here: 321 us
  waiting for transfers between devices  159 us (49%)
  matrix products  71.7 us (22%)
  local copies, waits for them, and re-layouts  65.4 us (20%)
  between operations  14 us (4%)
  other arithmetic  10.2 us (3%)
    reduce_scatter x2, waiting for transfers between devices, body(): lax.psum_scatter(jnp.einsum('tsa,tsb->sab', left_rows, right_cols, prefer...  123 us
    all_gather x1, waiting for transfers between devices, body(): lax.all_gather(own_weight, 'rep', axis=0, tiled=True)  36.9 us
    dot_general x12, matrix products, exact_dot(): return jnp.einsum('...ij,...jk->...ik', first, second)  29 us
    reshape x2, local copies, waits for them, and re-layouts, body(): grid = weights.reshape(row_blocks, block_size, col_blocks, block_size)  21.2 us
    dot_general x2, matrix products, body(): jnp.einsum('tsa,tsb->sab', left_rows, right_cols, preferred_element_type=...  19.6 us
    dot_general x1, matrix products, body(): jnp.einsum('tsa,sab->tsb', chosen, lax.all_gather(own_weight, 'rep', axis...  9.91 us
    gather x2, local copies, waits for them, and re-layouts, body(): right_cols = jnp.take(dgate_blocks, block_at % col_blocks, axis=1)  9.81 us
    gather x2, local copies, waits for them, and re-layouts, body(): left_rows = jnp.take(feature_blocks, block_at // col_blocks, axis=1)  9.76 us
  transfers between devices with their start and end apart: 3, of which 3 were waited for; matrix products, arithmetic and copies ran while one was open for 11% of the time, Pallas kernels for 0%

commit v1 on v0

--- a/solution.py
+++ b/solution.py
@@ -67,10 +67,17 @@
             gate_value = jnp.dot(features_now, weights, preferred_element_type=jnp.float32)
         else:
             chosen = jnp.take(feature_blocks, row_at, axis=1)
+
+            def time_pools_by_axis(target):
+                mixed_arr = lax.axis_size("rep")
+                part_now = jnp.stack([target] * mixed_arr)
+                seen_now = lax.all_to_all(part_now, "rep", 0, 0)
+                return jnp.concatenate(seen_now, 0)
+
             products = jnp.einsum(
                 "tsa,sab->tsb",
                 chosen,
-                lax.all_gather(own_weight, "rep", axis=0, tiled=True),
+                time_pools_by_axis(own_weight),
                 preferred_element_type=jnp.float32,
             )
             gate_value = jnp.einsum("tsb,sj->tjb", products, column_pick)

time: 322 us -> 372 us (1.16)
  waiting for transfers between devices: 159 us -> 200 us
  starting transfers between devices: 0.3 us -> 4.92 us
    all_to_all x0 -> x1, waiting for transfers between devices: none -> 77.6 us  [time_pools_by_axis(): seen_now = lax.all_to_all(part_now, 'rep', 0, 0)]
    all_gather x1 -> x0, waiting for transfers between devices: 36.9 us -> none  [body(): lax.all_gather(own_weight, 'rep', axis=0, tiled=True)]
    all_to_all x0 -> x1, starting transfers between devices: none -> 4.66 us  [time_pools_by_axis(): seen_now = lax.all_to_all(part_now, 'rep', 0, 0)]
  transfers between devices with their start and end apart: 3 -> 3, of which waited for: 3 -> 3; matrix products, arithmetic and copies ran while one was open for 11% -> 9% of each run, Pallas kernels for 0% -> 0%
where the time goes in v1:
time: 372 us; the launch traced here: 371 us
  waiting for transfers between devices  200 us (54%)
  matrix products  71.7 us (19%)
  local copies, waits for them, and re-layouts  69 us (19%)
  between operations  14.4 us (4%)
  other arithmetic  10.5 us (3%)
  starting transfers between devices  4.92 us (1%)
    reduce_scatter x2, waiting for transfers between devices, body(): lax.psum_scatter(jnp.einsum('tsa,tsb->sab', left_rows, right_cols, prefer...  122 us
    all_to_all x1, waiting for transfers between devices, time_pools_by_axis(): seen_now = lax.all_to_all(part_now, 'rep', 0, 0)  77.6 us
    dot_general x12, matrix products, exact_dot(): return jnp.einsum('...ij,...jk->...ik', first, second)  29 us
    reshape x2, local copies, waits for them, and re-layouts, body(): grid = weights.reshape(row_blocks, block_size, col_blocks, block_size)  21.2 us
    dot_general x2, matrix products, body(): jnp.einsum('tsa,tsb->sab', left_rows, right_cols, preferred_element_type=...  19.6 us
    gather x2, local copies, waits for them, and re-layouts, body(): right_cols = jnp.take(dgate_blocks, block_at % col_blocks, axis=1)  9.81 us
    gather x2, local copies, waits for them, and re-layouts, body(): left_rows = jnp.take(feature_blocks, block_at // col_blocks, axis=1)  9.76 us
    dot_general x1, matrix products, body(): jnp.einsum('tsa,sab->tsb', chosen, time_pools_by_axis(own_weight), prefer...  9.14 us
  transfers between devices with their start and end apart: 3, of which 3 were waited for; matrix products, arithmetic and copies ran while one was open for 9% of the time, Pallas kernels for 0%

profile of v1, /device:TPU:32, one launch (start us, length us, event | category | flops | bytes accessed | tf_op | source)
XLA Modules:
  0.0 370.6 jit_solution(13101057634628385193)
XLA Ops:
  7.2 0.8 select_reduce_fusion
  8.0 1.7 fusion.168
  9.7 0.5 copy.158
  10.2 0.5 copy.125
  10.8 5.4 %fusion.46 = bf16[256,1536]{1,0:T(8,128)(2,1)S(1)} fusion(bf16[2048,1536]{1,0:T(8,128)(2,1)} %param.13, bf16[2,256,1536]{2,1,0:T(8,128)(2,1)} %param.12, bf16[2,256,2048]{2,1,0:T(8,128)(2,1)} %param.11), kind=kOutput, calls=%fused_computation.43 | convolution fusion | flops 1614544896 | bytes 8912896 | tf_op jit(solution)/shard_map/dot_general | solution.py:67
  16.2 1.2 copy.126
  17.3 1.4 copy.127
  18.7 4.8 %gather_fusion.1 = bf16[48,256,256]{2,1,0:T(8,128)(2,1)} fusion(bf16[256,8,256]{2,0,1:T(8,128)(2,1)S(1)} %copy.125, s32[1024]{0:T(1024)S(1)} %pad_clamp_fusion.1), kind=kCustom, calls=%fused_computation.clone | custom fusion | bytes 12583104 | tf_op jit(solution)/shard_map/jit(_take)/gather | solution.py:89
  23.5 4.9 %gather_fusion.2 = bf16[48,256,256]{2,1,0:T(8,128)(2,1)} fusion(bf16[256,6,256]{2,0,1:T(8,128)(2,1)S(1)} %copy.127, s32[1024]{0:T(1024)S(1)} %pad_clamp_fusion), kind=kCustom, calls=%fused_computation.1.clone | custom fusion | bytes 12583104 | tf_op jit(solution)/shard_map/jit(_take)/gather | solution.py:90
  28.5 9.8 %fusion.17 = bf16[48,256,256]{2,1,0:T(8,128)(2,1)} fusion(bf16[48,256,256]{2,1,0:T(8,128)(2,1)} %gather_fusion.2, pred[48]{0:T(512)(128)(4,1)S(1)} %get-tuple-element.19, bf16[48,256,256]{2,1,0:T(8,128)(2,1)} %gather_fusion.1, pred[48]{0:T(512)(128)(4,1)S(1)} %get-tuple-element.8), kind=kOutput, calls=%fused_computation.21 | convolution fusion | flops 1620049920 | bytes 18874464 | tf_op jit(solution)/shard_map/tsa,tsb->sab/dot_general | solution.py:92
  38.3 13.4 %reshape.271 = bf16[8,256,6,256]{3,2,1,0:T(8,128)(2,1)} reshape(bf16[2048,1536]{1,0:T(8,128)(2,1)} %param.13) | data formatting | bytes 12582912 | tf_op jit(solution)/shard_map/reshape | solution.py:58
  51.7 7.8 %copy.123 = bf16[8,256,6,256]{3,1,2,0:T(8,128)(2,1)} copy(bf16[8,256,6,256]{3,2,1,0:T(8,128)(2,1)} %reshape.271) | data formatting | bytes 12582912 | tf_op jit(solution)/shard_map/reshape | solution.py:58
  59.7 3.5 gather_fusion
  63.1 51.7 %reduce-scatter.3.cloned.1.call-done = bf16[3,256,256]{2,1,0:T(8,128)(2,1)} async-done(((bf16[48,256,256]{2,1,0:T(8,128)(2,1)}), bf16[3,256,256]{2,1,0:T(8,128)(2,1)}) %reduce-scatter.3.cloned.1.call-update) | async-done | bytes 393232 | tf_op jit(solution)/shard_map/reduce_scatter | solution.py:91
  114.8 1.2 multiply_reduce_fusion.4
  116.0 2.4 multiply_reduce_fusion.3
  118.4 1.3 subtract_convert_fusion.1
  119.9 3.4 stack.49
  123.3 4.7 %all-to-all-start = ((bf16[16,3,256,256]{2,3,1,0:T(8,128)(2,1)}), bf16[16,3,256,256]{2,3,1,0:T(8,128)(2,1)}, u32[]{:S(2)}, u32[]{:S(2)}) async-start(bf16[16,3,256,256]{2,3,1,0:T(8,128)(2,1)} %stack.49), calls=%async_computation.1 | async-start | bytes 12582912 | tf_op jit(solution)/shard_map/all_to_all | solution.py:74
  128.2 0.5 copy.159
  128.7 0.5 copy.133
  129.3 4.9 %gather_fusion.3 = bf16[48,256,256]{2,1,0:T(8,128)(2,1)} fusion(bf16[256,8,256]{2,0,1:T(8,128)(2,1)S(1)} %copy.133, s32[1024]{0:T(1024)S(1)} %pad_clamp_fusion.1), kind=kCustom, calls=%fused_computation.2.clone | custom fusion | bytes 12583104 | tf_op jit(solution)/shard_map/jit(_take)/gather | solution.py:89
  134.7 77.6 %all-to-all-done = bf16[16,3,256,256]{2,3,1,0:T(8,128)(2,1)} async-done(((bf16[16,3,256,256]{2,3,1,0:T(8,128)(2,1)}), bf16[16,3,256,256]{2,3,1,0:T(8,128)(2,1)}, u32[]{:S(2)}, u32[]{:S(2)}) %all-to-all-start) | async-done | bytes 6291488 | tf_op jit(solution)/shard_map/all_to_all | solution.py:74
  212.4 9.1 %fusion.14 = bf16[256,48,256]{0,2,1:T(8,128)(2,1)} fusion(bf16[48,256,256]{1,2,0:T(8,128)(2,1)} %bitcast.14, bf16[48,256,256]{2,1,0:T(8,128)(2,1)} %gather_fusion.3, pred[48]{0:T(512)(128)(4,1)S(1)} %get-tuple-element.8), kind=kOutput, calls=%fused_computation.20 | convolution fusion | flops 1613758464 | bytes 18874416 | tf_op jit(solution)/shard_map/tsa,sab->tsb/dot_general | solution.py:77
  221.5 8.9 %copy.136 = bf16[256,48,256]{2,1,0:T(8,128)(2,1)} copy(bf16[256,48,256]{0,2,1:T(8,128)(2,1)} %fusion.14) | data formatting | bytes 12582912 | tf_op jit(solution)/shard_map/tsa,sab->tsb/transpose | solution.py:77
  230.4 3.7 fusion.144
  234.1 0.8 fusion.55
  234.9 4.9 %gather_fusion.4 = bf16[48,256,256]{2,1,0:T(8,128)(2,1)} fusion(bf16[256,6,256]{2,0,1:T(8,128)(2,1)S(1)} %fusion.55, s32[1024]{0:T(1024)S(1)} %pad_clamp_fusion), kind=kCustom, calls=%fused_computation.3.clone | custom fusion | bytes 12583104 | tf_op jit(solution)/shard_map/jit(_take)/gather | solution.py:90
  239.8 9.7 %fusion.22 = bf16[48,256,256]{2,1,0:T(8,128)(2,1)} fusion(bf16[48,256,256]{2,1,0:T(8,128)(2,1)} %gather_fusion.4, pred[48]{0:T(512)(128)(4,1)S(1)} %get-tuple-element.19, bf16[48,256,256]{2,1,0:T(8,128)(2,1)} %gather_fusion.3, pred[48]{0:T(512)(128)(4,1)S(1)} %get-tuple-element.8), kind=kOutput, calls=%fused_computation.22 | convolution fusion | flops 1620049920 | bytes 18874464 | tf_op jit(solution)/shard_map/tsa,tsb->sab/dot_general | solution.py:92
  249.6 0.6 copy-done.10
  250.5 0.7 fusion.141
  252.1 1.3 copy.143
  253.3 70.8 %reduce-scatter.5.cloned.1.call-done = bf16[3,256,256]{2,1,0:T(8,128)(2,1)} async-done(((bf16[48,256,256]{2,1,0:T(8,128)(2,1)}), bf16[3,256,256]{2,1,0:T(8,128)(2,1)}) %reduce-scatter.5.cloned.1.call-update) | async-done | bytes 393232 | tf_op jit(solution)/shard_map/reduce_scatter | solution.py:91
  324.1 1.6 fusion.172
  326.0 0.9 fusion.45
  327.0 1.2 copy.141
  329.5 0.7 copy-done.3
  331.2 1.8 fusion.32
  333.0 2.7 fusion.174
  335.7 5.1 %fusion.29 = bf16[6,256,256]{2,1,0:T(8,128)(2,1)} fusion(f32[6,256,256]{2,1,0:T(8,128)} %fusion.174, f32[256,256]{1,0:T(8,128)S(1)} %fusion.142), kind=kOutput, calls=%fused_computation.25 | convolution fusion | flops 403439616 | bytes 2621440 | tf_op jit(solution)/shard_map/...ij,...jk->...ik/dot_general | solution.py:14
  340.8 1.8 fusion.38
  342.6 2.7 fusion.171
  345.3 5.2 %fusion.35 = bf16[6,256,256]{2,1,0:T(8,128)(2,1)} fusion(f32[6,256,256]{2,1,0:T(8,128)} %fusion.171, f32[256,256]{1,0:T(8,128)S(1)} %fusion.142), kind=kOutput, calls=%fused_computation.29 | convolution fusion | flops 403439616 | bytes 2621440 | tf_op jit(solution)/shard_map/...ij,...jk->...ik/dot_general | solution.py:14
  350.5 4.1 %fusion.103 = bf16[6,256,256]{2,1,0:T(8,128)(2,1)} fusion(bf16[6,256,256]{2,1,0:T(8,128)(2,1)} %bitcast.160, bf16[6,256,256]{2,1,0:T(8,128)(2,1)} %fusion.35, f32[6,256,256]{2,1,0:T(8,128)} %fusion.171, f32[6,256,256]{2,1,0:T(8,128)S(1)} %get-tuple-element.13, f32[6]{0:T(128)S(1)} %power_multiply_fusion.1, f32[256,256]{1,0:T(8,128)S(1)} %fusion.142, ...), kind=kOutput, calls=%fused_computation.87 | convolution fusion | flops 607125504 | bytes 5767198 | tf_op jit(solution)/shard_map/...ij,...jk->...ik/dot_general | solution.py:14
  354.6 1.3 multiply_reduce_fusion.2
  355.9 2.5 multiply_reduce_fusion.1
  358.5 3.1 fusion.98
  361.6 2.1 fusion.140
  (58 shorter events, 4.9 us)
Async XLA Ops:
  7.2 107.6 %reduce-scatter.3.cloned.1.call-start = ((), (), s32[]{:S(2)}) async-start(), calls=%async_computation.3 | async-start | bytes 6684672 | tf_op jit(solution)/shard_map/reduce_scatter | solution.py:91
  38.3 13.4 %copy-start.6 = (bf16[1,3,2,256,256]{4,3,2,1,0:T(8,128)(2,1)S(1)}, bf16[1,3,2,256,256]{4,3,2,1,0:T(8,128)(2,1)}, u32[]{:S(2)}) copy-start(bf16[1,3,2,256,256]{4,3,2,1,0:T(8,128)(2,1)} %param.16) | copy-start | bytes 2359300
  119.7 3.5 copy-start.5
  123.3 89.1 %all-to-all-start = ((bf16[16,3,256,256]{2,3,1,0:T(8,128)(2,1)}), bf16[16,3,256,256]{2,3,1,0:T(8,128)(2,1)}, u32[]{:S(2)}, u32[]{:S(2)}) async-start(bf16[16,3,256,256]{2,3,1,0:T(8,128)(2,1)} %stack.49), calls=%async_computation.1 | async-start | bytes 12582912 | tf_op jit(solution)/shard_map/all_to_all | solution.py:74
  128.0 196.1 %reduce-scatter.5.cloned.1.call-start = ((), (), s32[]{:S(2)}) async-start(), calls=%async_computation.4 | async-start | bytes 6684672 | tf_op jit(solution)/shard_map/reduce_scatter | solution.py:91
  129.2 4.9 %slice-start = ((bf16[2,256,1536]{2,1,0:T(8,128)(2,1)}), bf16[1,256,1536]{2,1,0:T(8,128)(2,1)S(1)}, s32[]{:S(2)}) async-start(bf16[2,256,1536]{2,1,0:T(8,128)(2,1)} %param.12), calls=%async_computation.5 | async-start | bytes 1572864 | tf_op jit(solution)/shard_map/slice | solution.py:85
  249.6 0.7 copy-start.10
  249.6 1.7 copy-start
  324.1 1.6 copy-start.2
  324.1 1.9 copy-start.7
  324.1 1.9 copy-start.9
  328.6 1.0 copy-start.8
  328.8 1.4 copy-start.3
  328.8 1.9 copy-start.4
  354.6 3.9 %copy-start.1 = (f32[6,256,256]{2,1,0:T(8,128)S(1)}, f32[6,256,256]{2,1,0:T(8,128)}, u32[]{:S(2)}) copy-start(f32[6,256,256]{2,1,0:T(8,128)} %fusion.174) | copy-start | bytes 4718596
Sparse Core Ops, SparseCore 0:
  38.4 76.3 reduce-scatter.2
  249.7 74.3 reduce-scatter.4
